TPU v7x, 32 devices: a whole 2x2x4 slice. The times are simulated.
32 devices in a mesh: layer: 4 (over x, core), grid: 8 (over z, y).
Axes of the slice: x: 2, y: 2, z: 4, core: 2. Of those that a mesh axis runs over, the one named last changes fastest.
Arguments:
- fourier: float32 [1024, 512, 256], P(('layer', 'grid')), may hold values from -6 to 6
- weights: float32 [1024], P(('layer', 'grid')), may hold values from 0.009375 to 0.09375
- legendre: float32 [256, 513, 1024], P('grid'), may hold values from -6 to 6
- pair_slots: int32 [256], replicated, may hold values from 0 to 255, each once
Outputs:
- spectra: float32 [256, 513, 256], P('grid', None, 'layer')
Inputs may be any that keep to these rules, and one draw needn't show every extreme that they name: Each pair index appears exactly once; position q holds wavenumbers pair_slots[q] and 511 - pair_slots[q].
All inputs are finite; a program needn't handle non-finite values.
Results may differ from a plain program's by a relative error of at most 0.0003.
Values sent between devices are 32-bit elements; how exact they have to be, the bound alone decides.
A program may use at most 256 MiB of HBM per device.

v0:
```python
import jax
import jax.numpy as jnp
from jax import lax
from jax.sharding import PartitionSpec as P


def project(poly_block, values, limits):
    local_pairs = poly_block.shape[0]
    slots_view = values.reshape(values.shape[0], local_pairs, 2, values.shape[2])
    product = jnp.einsum(
        "qrl,lqsc->qrsc",
        poly_block,
        slots_view,
        precision=lax.Precision.HIGHEST,
        preferred_element_type=jnp.float32,
    )
    row_ids = jnp.arange(poly_block.shape[1], dtype=jnp.int32)
    in_first = row_ids[None, :] < limits[:, None]
    return jnp.where(in_first[:, :, None], product[:, :, 0, :], product[:, :, 1, :])


def shards(fourier, weights, legendre, pair_slots):
    pair_count = pair_slots.shape[0]
    waves = 2 * pair_count
    scaled = fourier * weights[:, None, None]
    seconds = waves - 1 - pair_slots
    slot_order = jnp.stack([pair_slots, seconds], axis=1).reshape(waves)
    packed = jnp.take(scaled, slot_order, axis=1)
    owned = lax.all_to_all(packed, "grid", split_axis=1, concat_axis=0, tiled=True)
    local_pairs = legendre.shape[0]
    own_pairs = lax.dynamic_slice_in_dim(
        pair_slots, lax.axis_index("grid") * local_pairs, local_pairs
    )
    limits = waves - own_pairs
    lat_rows = owned.shape[0]
    lat_block = lax.dynamic_slice_in_dim(legendre, lax.axis_index("layer") * lat_rows, lat_rows, 2)
    partial_value = project(lat_block, owned, limits)
    return lax.psum_scatter(partial_value, "layer", scatter_dimension=2, tiled=True)


def solution(mesh):
    in_specs = (P(("layer", "grid"), None, None), P(("layer", "grid")), P("grid", None, None), P())
    out_specs = P("grid", None, "layer")
    return jax.shard_map(shards, mesh=mesh, in_specs=in_specs, out_specs=out_specs, check_vma=False)
```

profile of v0, /device:TPU:0, one launch (start us, length us, event | category | flops | bytes accessed | tf_op | source)
XLA Modules:
  0.0 699.2 jit_solution(15030018687639173597)
XLA Ops:
  6.5 0.7 broadcast_subtract_fusion
  7.2 0.7 pad_add_fusion
  7.9 0.1 copy.17
  8.0 0.1 reshape.66
  8.2 0.1 reshape.65
  8.4 17.8 %copy_multiply_fusion = f32[32,512,256]{2,0,1:T(8,128)} fusion(f32[32,512,256]{2,1,0:T(8,128)} %param.4, f32[32]{0:T(128)} %param.5), kind=kLoop, calls=%fused_computation.6 | loop fusion | flops 4194304 | bytes 33554560 | tf_op jit(solution)/shard_map/mul | solution.py:25
  26.2 17.0 %gather_fusion = f32[512,32,256]{2,1,0:T(8,128)} fusion(f32[32,512,256]{2,0,1:T(8,128)} %copy_multiply_fusion, s32[1024]{0:T(1024)S(1)} %pad_clamp_fusion), kind=kCustom, calls=%fused_computation | custom fusion | bytes 33556480 | tf_op jit(solution)/shard_map/jit(_take)/gather | solution.py:28
  43.3 11.7 %select_bitcast_fusion = f32[32,512,256]{2,0,1:T(8,128)} fusion(f32[512,32,256]{2,1,0:T(8,128)} %gather_fusion, pred[512]{0:T(512)(128)(4,1)S(1)} %compare_and_fusion), kind=kLoop, calls=%fused_computation.7 | loop fusion | flops 4194304 | bytes 33554944 | tf_op jit(solution)/shard_map/jit(_take)/select_n | solution.py:28
  55.0 0.0 copy-start
  55.0 7.4 %all-to-all-start = ((f32[32,512,256]{2,0,1:T(8,128)}), f32[32,512,256]{2,0,1:T(8,128)}, u32[]{:S(2)}, u32[]{:S(2)}) async-start(f32[32,512,256]{2,0,1:T(8,128)} %select_bitcast_fusion), calls=%async_computation | async-start | bytes 33554432 | tf_op jit(solution)/shard_map/all_to_all | solution.py:29
  62.4 0.2 reduce-scatter.2.cloned.1.call-start
  62.6 0.0 copy-done
  62.6 0.1 dynamic-slice_subtract_fusion
  62.7 0.1 iota_compare_fusion
  62.8 11.4 %constant_dynamic-slice_fusion = f32[32,513,256]{2,0,1:T(8,128)} fusion(f32[32,513,1024]{2,0,1:T(8,128)} %param.6, s32[]{:T(128)S(6)} %select_n.31), kind=kLoop, calls=%fused_computation.16 | loop fusion | bytes 33619972 | tf_op jit(solution)/shard_map/dynamic_slice | solution.py:36
  74.2 351.2 %all-to-all-done = f32[32,512,256]{2,0,1:T(8,128)} async-done(((f32[32,512,256]{2,0,1:T(8,128)}), f32[32,512,256]{2,0,1:T(8,128)}, u32[]{:S(2)}, u32[]{:S(2)}) %all-to-all-start) | async-done | bytes 16777248 | tf_op jit(solution)/shard_map/all_to_all | solution.py:29
  425.4 11.8 %copy.20 = f32[32,8,64,256]{3,0,1,2:T(8,128)} copy(f32[32,8,64,256]{3,0,2,1:T(8,128)} %bitcast.6) | data formatting | bytes 33554432 | tf_op jit(solution)/shard_map/all_to_all | solution.py:29
  437.2 56.5 %fusion.1 = f32[32,513,2,256]{3,1,2,0:T(8,128)} fusion(f32[256,32,2,256]{3,0,2,1:T(8,128)} %bitcast.25, f32[32,513,256]{2,0,1:T(8,128)} %constant_dynamic-slice_fusion), kind=kOutput, calls=%fused_computation.5 | convolution fusion | flops 25820135424 | bytes 67207168 | tf_op jit(solution)/shard_map/qrl,lqsc->qrsc/dot_general | solution.py:10
  493.7 17.1 %fusion = f32[32,513,256]{2,1,0:T(8,128)} fusion(f32[32,513,2,256]{3,1,2,0:T(8,128)} %fusion.1, pred[32,513]{1,0:T(8,128)(4,1)S(1)} %iota_compare_fusion), kind=kLoop, calls=%fused_computation.2 | loop fusion | flops 4202496 | bytes 50446368 | tf_op jit(solution)/shard_map/jit(_where)/select_n | solution.py:19
  510.8 24.0 %copy.22 = f32[32,513,256]{1,0,2:T(8,128)} copy(f32[32,513,256]{2,1,0:T(8,128)} %fusion) | data formatting | bytes 33619968 | tf_op jit(solution)/shard_map/jit(_where)/select_n | solution.py:19
  534.8 0.0 reduce-scatter.2.cloned.1.call-update
  534.8 149.7 %reduce-scatter.2.cloned.1.call-done = f32[32,513,64]{1,0,2:T(8,128)} async-done(((f32[32,513,256]{1,0,2:T(8,128)}), f32[32,513,64]{1,0,2:T(8,128)}) %reduce-scatter.2.cloned.1.call-update) | async-done | bytes 4202512 | tf_op jit(solution)/shard_map/reduce_scatter | solution.py:38
  684.5 7.9 %copy.23 = f32[32,513,64]{1,2,0:T(8,128)} copy(f32[32,513,64]{1,0,2:T(8,128)} %reduce-scatter.2.cloned.1.call-done) | data formatting | bytes 8404992 | tf_op jit(solution)/shard_map/reduce_scatter | solution.py:38
  (3 shorter events, 0.0 us)
Async XLA Ops:
  55.0 7.7 %copy-start = (s32[256]{0:T(256)S(1)}, s32[256]{0:T(256)}, u32[]{:S(2)}) copy-start(s32[256]{0:T(256)} %param.7) | copy-start | bytes 3076
  55.0 370.4 %all-to-all-start = ((f32[32,512,256]{2,0,1:T(8,128)}), f32[32,512,256]{2,0,1:T(8,128)}, u32[]{:S(2)}, u32[]{:S(2)}) async-start(f32[32,512,256]{2,0,1:T(8,128)} %select_bitcast_fusion), calls=%async_computation | async-start | bytes 33554432 | tf_op jit(solution)/shard_map/all_to_all | solution.py:29
  62.4 622.1 %reduce-scatter.2.cloned.1.call-start = ((), (), s32[]{:S(2)}) async-start(), calls=%async_computation.2 | async-start | bytes 26214400 | tf_op jit(solution)/shard_map/reduce_scatter | solution.py:38
Sparse Core Ops, SparseCore 0:
  534.9 149.5 reduce-scatter.1
where the time goes:
time: 700 us; the launch traced here: 699 us
  waiting for transfers between devices  501 us (72%)
  local copies, waits for them, and re-layouts  72.5 us (10%)
  matrix products  56.5 us (8%)
  other arithmetic  48.2 us (7%)
  between operations  13.5 us (2%)
  starting transfers between devices  7.66 us (1%)
    all_to_all x1, waiting for transfers between devices, shards(): lax.all_to_all(packed, 'grid', split_axis=1, concat_axis=0, tiled=True)  351 us
    reduce_scatter x1, waiting for transfers between devices, shards(): lax.psum_scatter(partial_value, 'layer', scatter_dimension=2, tiled=True)  150 us
    dot_general x1, matrix products, project(): jnp.einsum('qrl,lqsc->qrsc', poly_block, slots_view, precision=lax.Precis...  56.5 us
    select_n x1, local copies, waits for them, and re-layouts, project(): jnp.where(in_first[:, :, None], product[:, :, 0, :], product[:, :, 1, :])  24 us
    mul x1, other arithmetic, shards(): scaled = fourier * weights[:, None, None]  17.8 us
    select_n x1, other arithmetic, project(): jnp.where(in_first[:, :, None], product[:, :, 0, :], product[:, :, 1, :])  17.1 us
    gather x1, local copies, waits for them, and re-layouts, shards(): packed = jnp.take(scaled, slot_order, axis=1)  17 us
  transfers between devices with their start and end apart: 2, of which 2 were waited for; matrix products, arithmetic and copies ran while one was open for 2% of the time, Pallas kernels for 0%

commit v1 on v0

v1 whole, which is shorter than its diff:
```python
import functools

import jax
import jax.numpy as jnp
from jax import lax
from jax.experimental import pallas as pl
from jax.experimental.pallas import tpu as pltpu
from jax.sharding import PartitionSpec as P

CHUNKS = (1, 6, 1)
LANES = 128


def pack_kernel(waves, half, slots_ref, x_ref, w_ref, *rest):
    o_ref = rest[-1]
    rows = w_ref.shape[0]
    scale = w_ref[...]
    in_low = lax.broadcasted_iota(jnp.int32, (rows, LANES), 1) < half

    def step(q, carry):
        a = slots_ref[q]
        first = x_ref[pl.ds(a, rows, stride=waves), :] * scale
        second = x_ref[pl.ds(waves - 1 - a, rows, stride=waves), :] * scale
        o_ref[0, q] = jnp.where(in_low, first, pltpu.roll(second, half, 1))
        o_ref[1, q] = jnp.where(in_low, pltpu.roll(first, half, 1), second)
        return carry

    lax.fori_loop(0, o_ref.shape[1], step, 0, unroll=8)


def pack(fourier, weights, slots, layers, after):
    lats, waves, fields = fourier.shape
    pairs = slots.shape[0]
    flat = fourier.reshape(lats * waves, fields)
    wide = jnp.broadcast_to(weights[:, None], (lats, LANES))
    tile = 8
    return pl.pallas_call(
        functools.partial(pack_kernel, waves, fields // layers),
        grid_spec=pltpu.PrefetchScalarGridSpec(
            num_scalar_prefetch=1,
            grid=(fields // LANES, lats // tile),
            in_specs=[
                pl.BlockSpec((tile * waves, LANES), lambda c, i, s: (i, c)),
                pl.BlockSpec((tile, LANES), lambda c, i, s: (i, 0)),
            ]
            + [pl.BlockSpec(memory_space=pl.ANY)] * len(after),
            out_specs=pl.BlockSpec((2, pairs, tile, LANES), lambda c, i, s: (c, 0, i, 0)),
        ),
        out_shape=jax.ShapeDtypeStruct((layers, pairs, lats, LANES), jnp.float32),
        compiler_params=pltpu.CompilerParams(vmem_limit_bytes=56 * 2**20),
        cost_estimate=pl.CostEstimate(flops=fourier.size * 4, bytes_accessed=fourier.size * 4 * 4, transcendentals=0),
        name="pack",
    )(slots, flat, wide, *after)


def split(x):
    high = x.astype(jnp.bfloat16)
    return high, (x - high.astype(jnp.float32)).astype(jnp.bfloat16)


def project_kernel(limit_ref, poly_ref, x_ref, *rest):
    o_ref = rest[-1]
    half = o_ref.shape[1]
    limit = limit_ref[pl.program_id(0)]
    x = x_ref[...].reshape(-1, LANES)
    right = jnp.concatenate(split(x), axis=1)
    high, low = split(poly_ref[0])
    product = jnp.dot(high, right, preferred_element_type=jnp.float32)
    product = product + jnp.dot(low, right, preferred_element_type=jnp.float32)
    total = (product[:, :LANES] + product[:, LANES:]).T
    rows = lax.broadcasted_iota(jnp.int32, (half, total.shape[1]), 1)
    o_ref[0] = jnp.where(rows < limit, total[:half], total[half:])


def project(legendre, owned, limits, start, so_far):
    pairs, degrees, lats = legendre.shape
    sources, count, part, _ = owned.shape
    half = LANES // 2
    in_specs = [
        pl.BlockSpec((1, degrees, lats), lambda q, s: (q + start, 0, 0)),
        pl.BlockSpec((sources, 1, part, LANES), lambda q, s: (0, q, 0, 0)),
    ]
    operands = [limits, legendre, owned]
    aliases = {}
    if so_far is not None:
        in_specs.append(pl.BlockSpec(memory_space=pl.ANY))
        operands.append(so_far)
        aliases = {3: 0}
    return pl.pallas_call(
        project_kernel,
        grid_spec=pltpu.PrefetchScalarGridSpec(
            num_scalar_prefetch=1,
            grid=(count,),
            in_specs=in_specs,
            out_specs=pl.BlockSpec((1, half, degrees), lambda q, s: (q + start, 0, 0)),
        ),
        out_shape=jax.ShapeDtypeStruct((pairs, half, degrees), jnp.float32),
        input_output_aliases=aliases,
        compiler_params=pltpu.CompilerParams(vmem_limit_bytes=56 * 2**20),
        cost_estimate=pl.CostEstimate(
            flops=count * degrees * lats * 1024, bytes_accessed=count * degrees * lats * 8, transcendentals=0
        ),
        name="project",
    )(*operands)


def shards(layers, grids, fourier, weights, legendre, pair_slots):
    local_pairs = legendre.shape[0]
    waves = 2 * pair_slots.shape[0]
    by_owner = pair_slots.reshape(grids, local_pairs)
    limits = waves - lax.dynamic_index_in_dim(by_owner, lax.axis_index("grid"), 0, keepdims=False)
    lats = fourier.shape[0]
    unit = local_pairs // sum(CHUNKS)
    start, outs = 0, [None]
    for step, size in enumerate(CHUNKS):
        count = size * unit
        chunk = by_owner[:, start : start + count].reshape(-1)
        packed = pack(fourier, weights, chunk, layers, [legendre, outs[step - 1]] if step > 1 else [])
        packed = packed.reshape(layers * grids, count, lats, LANES)
        owned = lax.all_to_all(packed, ("layer", "grid"), split_axis=0, concat_axis=0, tiled=True)
        outs.append(project(legendre, owned, limits[start : start + count], start, outs[-1]))
        start += count
    return outs[-1].transpose(0, 2, 1)


def solution(mesh):
    in_specs = (P(("layer", "grid"), None, None), P(("layer", "grid")), P("grid", None, None), P())
    out_specs = P("grid", None, "layer")
    body = functools.partial(shards, mesh.shape["layer"], mesh.shape["grid"])
    return jax.shard_map(body, mesh=mesh, in_specs=in_specs, out_specs=out_specs, check_vma=False)
```

time: 700 us -> 422 us (0.60)
  waiting for transfers between devices: 501 us -> 249 us
  Pallas kernels: 0 us -> 103 us
  matrix products: 56.5 us -> 0 us
  other arithmetic: 48.2 us -> 0.01 us
  local copies, waits for them, and re-layouts: 72.5 us -> 54.4 us
  between operations: 13.5 us -> 0.04 us
    reduce_scatter x1 -> x0, waiting for transfers between devices: 150 us -> none  [shards(): lax.psum_scatter(partial_value, 'layer', scatter_dimension=2, tiled=True)]
    pallas_call x0 -> x6, Pallas kernels: none -> 103 us  [the longest x3 53.3 us: pack(): pl.pallas_call(functools.partial(pack_kernel, waves, fields // layers), g...]
    all_to_all x1 -> x3, waiting for transfers between devices: 351 us -> 249 us  [shards(): lax.all_to_all(packed, ('layer', 'grid'), split_axis=0, concat_axis=0, ti...]
    dot_general x1 -> x0, matrix products: 56.5 us -> none  [project(): jnp.einsum('qrl,lqsc->qrsc', poly_block, slots_view, precision=lax.Precis...]
    unnamed x2 -> x5, local copies, waits for them, and re-layouts: 0.01 us -> 49 us
    select_n x3 -> x0, other arithmetic: 28.8 us -> none  [the longest x1 17.1 us: project(): jnp.where(in_first[:, :, None], product[:, :, 0, :], product[:, :, 1, :])]
    select_n x1 -> x0, local copies, waits for them, and re-layouts: 24 us -> none  [project(): jnp.where(in_first[:, :, None], product[:, :, 0, :], product[:, :, 1, :])]
    mul x1 -> x0, other arithmetic: 17.8 us -> none  [shards(): scaled = fourier * weights[:, None, None]]
  transfers between devices with their start and end apart: 2 -> 3, of which waited for: 2 -> 3; matrix products, arithmetic and copies ran while one was open for 2% -> 12% of each run, Pallas kernels for 0% -> 20%
where the time goes in v1:
time: 422 us; the launch traced here: 421 us
  waiting for transfers between devices  249 us (59%)
  Pallas kernels  103 us (24%)
  local copies, waits for them, and re-layouts  54.4 us (13%)
  starting transfers between devices  13.8 us (3%)
    all_to_all x3, waiting for transfers between devices, shards(): lax.all_to_all(packed, ('layer', 'grid'), split_axis=0, concat_axis=0, ti...  249 us
    pallas_call x3, Pallas kernels, pack(): pl.pallas_call(functools.partial(pack_kernel, waves, fields // layers), g...  53.3 us
    pallas_call x3, Pallas kernels, project(): pl.pallas_call(project_kernel, grid_spec=pltpu.PrefetchScalarGridSpec(num...  50.1 us
    unnamed x5, local copies, waits for them, and re-layouts  49 us
    all_to_all x3, starting transfers between devices, shards(): lax.all_to_all(packed, ('layer', 'grid'), split_axis=0, concat_axis=0, ti...  13.8 us
  transfers between devices with their start and end apart: 3, of which 3 were waited for; matrix products, arithmetic and copies ran while one was open for 12% of the time, Pallas kernels for 20%

profile of v1, /device:TPU:0, one launch (start us, length us, event | category | flops | bytes accessed | tf_op | source)
XLA Modules:
  0.0 420.8 jit_solution(7342097541738209023)
XLA Ops:
  0.0 0.8 reshape.32
  0.8 0.1 fusion
  0.8 0.6 reshape.35.slots_ref
  1.5 1.3 broadcast_in_dim.2.w_ref
  2.8 11.4 %pack.3 = f32[4,32,32,128]{3,2,1,0:T(8,128)} custom-call(s32[32]{0:T(128)} %reshape.35.slots_ref, f32[16384,256]{1,0:T(8,128)} %bitcast.11, f32[32,128]{1,0:T(8,128)} %broadcast_in_dim.2.w_ref), custom_call_target="tpu_custom_call" | custom-call | flops 16777216 | bytes 67108864 | tf_op jit(solution)/shard_map/pack/pallas_call | solution.py:37
  14.2 7.3 %all-to-all-start = ((f32[32,4,32,128]{3,2,1,0:T(8,128)}), f32[32,4,32,128]{3,2,1,0:T(8,128)S(1)}, u32[]{:S(2)}, u32[]{:S(2)}) async-start(f32[32,4,32,128]{3,2,1,0:T(8,128)} %bitcast.16), calls=%async_computation | async-start | bytes 4194304 | tf_op jit(solution)/shard_map/all_to_all | solution.py:120
  21.6 0.1 slice.35
  21.6 0.7 reshape.38.slots_ref
  22.3 30.4 %pack.5 = f32[4,192,32,128]{3,2,1,0:T(8,128)} custom-call(s32[192]{0:T(256)} %reshape.38.slots_ref, f32[16384,256]{1,0:T(8,128)} %bitcast.12, f32[32,128]{1,0:T(8,128)} %broadcast_in_dim.2.w_ref), custom_call_target="tpu_custom_call" | custom-call | flops 16777216 | bytes 67108864 | tf_op jit(solution)/shard_map/pack/pallas_call | solution.py:37
  52.7 18.9 %all-to-all-done.x_ref = f32[32,4,32,128]{3,2,1,0:T(8,128)S(1)} async-done(((f32[32,4,32,128]{3,2,1,0:T(8,128)}), f32[32,4,32,128]{3,2,1,0:T(8,128)S(1)}, u32[]{:S(2)}, u32[]{:S(2)}) %all-to-all-start) | async-done | bytes 2097184 | tf_op jit(solution)/shard_map/all_to_all | solution.py:120
  71.6 0.0 copy-start
  71.6 1.3 copy-done
  72.9 3.8 all-to-all-start.2
  76.7 0.6 reshape.33.slots_ref
  77.3 46.4 %copy.14.poly_ref.rest_0_ = f32[32,513,1024]{2,1,0:T(8,128)} copy(f32[32,513,1024]{2,0,1:T(8,128)} %param.6) | data formatting | bytes 134479872 | tf_op args[2]
  123.7 0.6 slice_bitcast_fusion.1
  124.3 7.5 %project.3.rest_1_.rest_0_ = f32[32,64,513]{2,1,0:T(8,128)} custom-call(s32[4]{0:T(128)} %get-tuple-element.7.limit_ref, f32[32,513,1024]{2,1,0:T(8,128)} %copy.14.poly_ref.rest_0_, f32[32,4,32,128]{3,2,1,0:T(8,128)} %copy-done), custom_call_target="tpu_custom_call" | custom-call | flops 2151677952 | bytes 16809984 | tf_op jit(solution)/shard_map/project/pallas_call | solution.py:89
  131.9 11.5 %pack.4 = f32[4,32,32,128]{3,2,1,0:T(8,128)} custom-call(s32[32]{0:T(128)} %reshape.33.slots_ref, f32[16384,256]{1,0:T(8,128)} %bitcast.13, f32[32,128]{1,0:T(8,128)} %broadcast_in_dim.2.w_ref, f32[32,513,1024]{2,1,0:T(8,128)} %copy.14.poly_ref.rest_0_, f32[32,64,513]{2,1,0:T(8,128)} %project.3.rest_1_.rest_0_), custom_call_target="tpu_custom_call" | custom-call | flops 16777216 | bytes 67108864 | tf_op jit(solution)/shard_map/pack/pallas_call | solution.py:37
  143.3 215.9 %all-to-all-done.2.x_ref = f32[32,24,32,128]{3,2,1,0:T(8,128)} async-done(((f32[32,24,32,128]{3,2,1,0:T(8,128)}), f32[32,24,32,128]{3,2,1,0:T(8,128)}, u32[]{:S(2)}, u32[]{:S(2)}) %all-to-all-start.2) | async-done | bytes 12582944 | tf_op jit(solution)/shard_map/all_to_all | solution.py:120
  359.2 2.7 all-to-all-start.1
  361.9 0.7 slice_bitcast_fusion.limit_ref
  362.6 35.1 %project.4.rest_0_ = f32[32,64,513]{2,1,0:T(8,128)} custom-call(s32[24]{0:T(128)} %slice_bitcast_fusion.limit_ref, f32[32,513,1024]{2,1,0:T(8,128)} %copy.14.poly_ref.rest_0_, f32[32,24,32,128]{3,2,1,0:T(8,128)} %all-to-all-done.2.x_ref, f32[32,64,513]{2,1,0:T(8,128)} %project.3.rest_1_.rest_0_), custom_call_target="tpu_custom_call", output_to_operand_aliasing={{}: (3, {})} | custom-call | flops 12910067712 | bytes 100859904 | tf_op jit(solution)/shard_map/project/pallas_call | solution.py:89
  397.7 14.3 %all-to-all-done.1.x_ref = f32[32,4,32,128]{3,2,1,0:T(8,128)S(1)} async-done(((f32[32,4,32,128]{3,2,1,0:T(8,128)}), f32[32,4,32,128]{3,2,1,0:T(8,128)S(1)}, u32[]{:S(2)}, u32[]{:S(2)}) %all-to-all-start.1) | async-done | bytes 2097184 | tf_op jit(solution)/shard_map/all_to_all | solution.py:120
  412.0 0.0 copy-start.1
  412.0 1.3 copy-done.1
  413.3 7.5 %project.5 = f32[32,64,513]{2,1,0:T(8,128)} custom-call(s32[4]{0:T(128)} %get-tuple-element.8.limit_ref, f32[32,513,1024]{2,1,0:T(8,128)} %copy.14.poly_ref.rest_0_, f32[32,4,32,128]{3,2,1,0:T(8,128)} %copy-done.1, f32[32,64,513]{2,1,0:T(8,128)} %project.4.rest_0_), custom_call_target="tpu_custom_call", output_to_operand_aliasing={{}: (3, {})} | custom-call | flops 2151677952 | bytes 16809984 | tf_op jit(solution)/shard_map/project/pallas_call | solution.py:89
  (1 shorter events, 0.0 us)
Async XLA Ops:
  14.2 57.4 %all-to-all-start = ((f32[32,4,32,128]{3,2,1,0:T(8,128)}), f32[32,4,32,128]{3,2,1,0:T(8,128)S(1)}, u32[]{:S(2)}, u32[]{:S(2)}) async-start(f32[32,4,32,128]{3,2,1,0:T(8,128)} %bitcast.16), calls=%async_computation | async-start | bytes 4194304 | tf_op jit(solution)/shard_map/all_to_all | solution.py:120
  71.6 1.3 copy-start
  72.9 286.3 %all-to-all-start.2 = ((f32[32,24,32,128]{3,2,1,0:T(8,128)}), f32[32,24,32,128]{3,2,1,0:T(8,128)}, u32[]{:S(2)}, u32[]{:S(2)}) async-start(f32[32,24,32,128]{3,2,1,0:T(8,128)} %bitcast.14), calls=%async_computation.2 | async-start | bytes 25165824 | tf_op jit(solution)/shard_map/all_to_all | solution.py:120
  359.2 52.8 %all-to-all-start.1 = ((f32[32,4,32,128]{3,2,1,0:T(8,128)}), f32[32,4,32,128]{3,2,1,0:T(8,128)S(1)}, u32[]{:S(2)}, u32[]{:S(2)}) async-start(f32[32,4,32,128]{3,2,1,0:T(8,128)} %bitcast.15), calls=%async_computation.1 | async-start | bytes 4194304 | tf_op jit(solution)/shard_map/all_to_all | solution.py:120
  412.0 1.3 copy-start.1

commit v2 on v1

--- a/solution.py
+++ b/solution.py
@@ -7,20 +7,51 @@
 from jax.experimental.pallas import tpu as pltpu
 from jax.sharding import PartitionSpec as P
 
-CHUNKS = (1, 6, 1)
 LANES = 128
 
 
-def pack_kernel(waves, half, slots_ref, x_ref, w_ref, *rest):
-    o_ref = rest[-1]
-    rows = w_ref.shape[0]
-    scale = w_ref[...]
+def pack_kernel(waves, half, local_pairs, begin, count, rows, slots_ref, x_ref, w_ref, *rest):
+    o_ref, held, sem = rest[-3:]
+    pitch = held.shape[1] // rows
+    tiles = pl.num_programs(1)
+    now = pl.program_id(0) * tiles + pl.program_id(1)
+    last = pl.num_programs(0) * tiles - 1
+
+    def copies(index, slot):
+        columns = pl.ds(pl.multiple_of(index // tiles * LANES, LANES), LANES)
+        for row in range(rows):
+            start = pl.multiple_of((index % tiles * rows + row) * waves, 8)
+            yield pltpu.make_async_copy(
+                x_ref.at[pl.ds(start, waves), columns],
+                held.at[slot, pl.ds(row * pitch, waves)],
+                sem.at[slot, row],
+            )
+
+    @pl.when(now == 0)
+    def _():
+        for copy in copies(now, 0):
+            copy.start()
+
+    @pl.when(now < last)
+    def _():
+        for copy in copies(now + 1, (now + 1) % 2):
+            copy.start()
+
+    slot = now % 2
+    for copy in copies(now, slot):
+        copy.wait()
+
+    x = held.at[slot]
+    row_ids = lax.broadcasted_iota(jnp.int32, (rows, LANES), 0)
+    scale = jnp.zeros((rows, LANES), jnp.float32)
+    for row in range(rows):
+        scale = jnp.where(row_ids == row, w_ref[pl.program_id(1) * rows + row], scale)
     in_low = lax.broadcasted_iota(jnp.int32, (rows, LANES), 1) < half
 
     def step(q, carry):
-        a = slots_ref[q]
-        first = x_ref[pl.ds(a, rows, stride=waves), :] * scale
-        second = x_ref[pl.ds(waves - 1 - a, rows, stride=waves), :] * scale
+        a = slots_ref[q // count * local_pairs + begin + q % count]
+        first = x[pl.ds(a, rows, stride=pitch), :] * scale
+        second = x[pl.ds(waves - 1 - a, rows, stride=pitch), :] * scale
         o_ref[0, q] = jnp.where(in_low, first, pltpu.roll(second, half, 1))
         o_ref[1, q] = jnp.where(in_low, pltpu.roll(first, half, 1), second)
         return carry
@@ -28,29 +59,33 @@
     lax.fori_loop(0, o_ref.shape[1], step, 0, unroll=8)
 
 
-def pack(fourier, weights, slots, layers, after):
+def pack(fourier, weights, slots, layers, grids, begin, count, after):
     lats, waves, fields = fourier.shape
-    pairs = slots.shape[0]
+    pairs = grids * count
+    local_pairs = slots.shape[0] // grids
     flat = fourier.reshape(lats * waves, fields)
-    wide = jnp.broadcast_to(weights[:, None], (lats, LANES))
     tile = 8
     return pl.pallas_call(
-        functools.partial(pack_kernel, waves, fields // layers),
+        functools.partial(pack_kernel, waves, fields // layers, local_pairs, begin, count, tile),
         grid_spec=pltpu.PrefetchScalarGridSpec(
             num_scalar_prefetch=1,
             grid=(fields // LANES, lats // tile),
             in_specs=[
-                pl.BlockSpec((tile * waves, LANES), lambda c, i, s: (i, c)),
-                pl.BlockSpec((tile, LANES), lambda c, i, s: (i, 0)),
+                pl.BlockSpec(memory_space=pl.ANY),
+                pl.BlockSpec(memory_space=pltpu.SMEM),
             ]
             + [pl.BlockSpec(memory_space=pl.ANY)] * len(after),
             out_specs=pl.BlockSpec((2, pairs, tile, LANES), lambda c, i, s: (c, 0, i, 0)),
+            scratch_shapes=[
+                pltpu.VMEM((2, tile * (waves + 8), LANES), jnp.float32),
+                pltpu.SemaphoreType.DMA((2, tile)),
+            ],
         ),
         out_shape=jax.ShapeDtypeStruct((layers, pairs, lats, LANES), jnp.float32),
         compiler_params=pltpu.CompilerParams(vmem_limit_bytes=56 * 2**20),
         cost_estimate=pl.CostEstimate(flops=fourier.size * 4, bytes_accessed=fourier.size * 4 * 4, transcendentals=0),
         name="pack",
-    )(slots, flat, wide, *after)
+    )(slots, flat, weights, *after)
 
 
 def split(x):
@@ -110,12 +145,11 @@
     by_owner = pair_slots.reshape(grids, local_pairs)
     limits = waves - lax.dynamic_index_in_dim(by_owner, lax.axis_index("grid"), 0, keepdims=False)
     lats = fourier.shape[0]
-    unit = local_pairs // sum(CHUNKS)
+    first, last = max(1, local_pairs // 8), max(1, local_pairs * 3 // 32)
     start, outs = 0, [None]
-    for step, size in enumerate(CHUNKS):
-        count = size * unit
-        chunk = by_owner[:, start : start + count].reshape(-1)
-        packed = pack(fourier, weights, chunk, layers, [legendre, outs[step - 1]] if step > 1 else [])
+    for step, count in enumerate((first, local_pairs - first - last, last)):
+        after = [legendre, outs[step - 1]] if step > 1 else []
+        packed = pack(fourier, weights, pair_slots, layers, grids, start, count, after)
         packed = packed.reshape(layers * grids, count, lats, LANES)
         owned = lax.all_to_all(packed, ("layer", "grid"), split_axis=0, concat_axis=0, tiled=True)
         outs.append(project(legendre, owned, limits[start : start + count], start, outs[-1]))

time: 422 us -> 419 us (level)
    unnamed x5 -> x7, local copies, waits for them, and re-layouts: 49 us -> 48.9 us
where the time goes in v2:
time: 419 us; the launch traced here: 417 us
  waiting for transfers between devices  250 us (60%)
  Pallas kernels  103 us (25%)
  local copies, waits for them, and re-layouts  50.9 us (12%)
  starting transfers between devices  13.8 us (3%)
    all_to_all x3, waiting for transfers between devices, shards(): lax.all_to_all(packed, ('layer', 'grid'), split_axis=0, concat_axis=0, ti...  250 us
    pallas_call x3, Pallas kernels, pack(): pl.pallas_call(functools.partial(pack_kernel, waves, fields // layers, lo...  52.5 us
    pallas_call x3, Pallas kernels, project(): pl.pallas_call(project_kernel, grid_spec=pltpu.PrefetchScalarGridSpec(num...  50.4 us
    unnamed x7, local copies, waits for them, and re-layouts  48.9 us
    all_to_all x3, starting transfers between devices, shards(): lax.all_to_all(packed, ('layer', 'grid'), split_axis=0, concat_axis=0, ti...  13.8 us
  transfers between devices with their start and end apart: 3, of which 3 were waited for; matrix products, arithmetic and copies ran while one was open for 12% of the time, Pallas kernels for 20%

profile of v2, /device:TPU:0, one launch (start us, length us, event | category | flops | bytes accessed | tf_op | source)
XLA Modules:
  0.0 417.4 jit_solution(5666314633281786844)
XLA Ops:
  0.0 11.6 %pack.3 = f32[4,32,32,128]{3,2,1,0:T(8,128)} custom-call(s32[256]{0:T(256)} %slots_ref.5, f32[16384,256]{1,0:T(8,128)} %bitcast.11, f32[32]{0:T(128)} %w_ref.5), custom_call_target="tpu_custom_call" | custom-call | flops 16777216 | bytes 67108864 | tf_op jit(solution)/shard_map/pack/pallas_call | solution.py:68
  11.6 7.3 %all-to-all-start = ((f32[32,4,32,128]{3,2,1,0:T(8,128)}), f32[32,4,32,128]{3,2,1,0:T(8,128)S(1)}, u32[]{:S(2)}, u32[]{:S(2)}) async-start(f32[32,4,32,128]{3,2,1,0:T(8,128)} %bitcast.15), calls=%async_computation | async-start | bytes 4194304 | tf_op jit(solution)/shard_map/all_to_all | solution.py:154
  19.0 29.7 %pack.5 = f32[4,200,32,128]{3,2,1,0:T(8,128)} custom-call(s32[256]{0:T(256)} %slots_ref.5, f32[16384,256]{1,0:T(8,128)} %bitcast.12, f32[32]{0:T(128)} %w_ref.5), custom_call_target="tpu_custom_call" | custom-call | flops 16777216 | bytes 67108864 | tf_op jit(solution)/shard_map/pack/pallas_call | solution.py:68
  48.7 20.4 %all-to-all-done.x_ref = f32[32,4,32,128]{3,2,1,0:T(8,128)S(1)} async-done(((f32[32,4,32,128]{3,2,1,0:T(8,128)}), f32[32,4,32,128]{3,2,1,0:T(8,128)S(1)}, u32[]{:S(2)}, u32[]{:S(2)}) %all-to-all-start) | async-done | bytes 2097184 | tf_op jit(solution)/shard_map/all_to_all | solution.py:154
  69.0 0.0 copy-start
  69.0 0.0 copy-start.2
  69.0 1.4 copy-done
  70.4 3.8 all-to-all-start.2
  74.2 0.0 copy-done.2
  74.2 0.1 reshape.22
  74.3 46.4 %copy.10.poly_ref.rest_0_ = f32[32,513,1024]{2,1,0:T(8,128)} copy(f32[32,513,1024]{2,0,1:T(8,128)} %param.6) | data formatting | bytes 134479872 | tf_op args[2]
  120.7 0.6 slice_bitcast_fusion.1.limit_ref
  121.3 7.5 %project.3.rest_1_.rest_0_ = f32[32,64,513]{2,1,0:T(8,128)} custom-call(s32[4]{0:T(128)} %slice_bitcast_fusion.1.limit_ref, f32[32,513,1024]{2,1,0:T(8,128)} %copy.10.poly_ref.rest_0_, f32[32,4,32,128]{3,2,1,0:T(8,128)} %copy-done), custom_call_target="tpu_custom_call" | custom-call | flops 2151677952 | bytes 16809984 | tf_op jit(solution)/shard_map/project/pallas_call | solution.py:124
  128.8 11.2 %pack.4 = f32[4,24,32,128]{3,2,1,0:T(8,128)} custom-call(s32[256]{0:T(256)} %slots_ref.5, f32[16384,256]{1,0:T(8,128)} %bitcast.13, f32[32]{0:T(128)} %w_ref.5, f32[32,513,1024]{2,1,0:T(8,128)} %copy.10.poly_ref.rest_0_, f32[32,64,513]{2,1,0:T(8,128)} %project.3.rest_1_.rest_0_), custom_call_target="tpu_custom_call" | custom-call | flops 16777216 | bytes 67108864 | tf_op jit(solution)/shard_map/pack/pallas_call | solution.py:68
  140.0 228.2 %all-to-all-done.2.x_ref = f32[32,25,32,128]{3,2,1,0:T(8,128)} async-done(((f32[32,25,32,128]{3,2,1,0:T(8,128)}), f32[32,25,32,128]{3,2,1,0:T(8,128)}, u32[]{:S(2)}, u32[]{:S(2)}) %all-to-all-start.2) | async-done | bytes 13107232 | tf_op jit(solution)/shard_map/all_to_all | solution.py:154
  368.2 2.7 all-to-all-start.1
  370.9 0.7 slice_bitcast_fusion.limit_ref
  371.6 0.6 slice_bitcast_fusion.2.limit_ref
  372.2 36.5 %project.4.rest_0_ = f32[32,64,513]{2,1,0:T(8,128)} custom-call(s32[25]{0:T(128)} %slice_bitcast_fusion.limit_ref, f32[32,513,1024]{2,1,0:T(8,128)} %copy.10.poly_ref.rest_0_, f32[32,25,32,128]{3,2,1,0:T(8,128)} %all-to-all-done.2.x_ref, f32[32,64,513]{2,1,0:T(8,128)} %project.3.rest_1_.rest_0_), custom_call_target="tpu_custom_call", output_to_operand_aliasing={{}: (3, {})} | custom-call | flops 13447987200 | bytes 105062400 | tf_op jit(solution)/shard_map/project/pallas_call | solution.py:124
  408.7 1.0 all-to-all-done.1.x_ref
  409.7 0.0 copy-start.1
  409.7 1.2 copy-done.1
  410.9 6.5 %project.5 = f32[32,64,513]{2,1,0:T(8,128)} custom-call(s32[3]{0:T(128)} %slice_bitcast_fusion.2.limit_ref, f32[32,513,1024]{2,1,0:T(8,128)} %copy.10.poly_ref.rest_0_, f32[32,3,32,128]{3,2,1,0:T(8,128)} %copy-done.1, f32[32,64,513]{2,1,0:T(8,128)} %project.4.rest_0_), custom_call_target="tpu_custom_call", output_to_operand_aliasing={{}: (3, {})} | custom-call | flops 1613758464 | bytes 12607488 | tf_op jit(solution)/shard_map/project/pallas_call | solution.py:124
  (1 shorter events, 0.0 us)
Async XLA Ops:
  11.6 57.4 %all-to-all-start = ((f32[32,4,32,128]{3,2,1,0:T(8,128)}), f32[32,4,32,128]{3,2,1,0:T(8,128)S(1)}, u32[]{:S(2)}, u32[]{:S(2)}) async-start(f32[32,4,32,128]{3,2,1,0:T(8,128)} %bitcast.15), calls=%async_computation | async-start | bytes 4194304 | tf_op jit(solution)/shard_map/all_to_all | solution.py:154
  69.0 1.4 copy-start
  69.0 5.2 %copy-start.2 = (s32[256]{0:T(256)S(1)}, s32[256]{0:T(256)}, u32[]{:S(2)}) copy-start(s32[256]{0:T(256)} %slots_ref.5) | copy-start | bytes 3076
  70.4 297.8 %all-to-all-start.2 = ((f32[32,25,32,128]{3,2,1,0:T(8,128)}), f32[32,25,32,128]{3,2,1,0:T(8,128)}, u32[]{:S(2)}, u32[]{:S(2)}) async-start(f32[32,25,32,128]{3,2,1,0:T(8,128)} %bitcast.14), calls=%async_computation.2 | async-start | bytes 26214400 | tf_op jit(solution)/shard_map/all_to_all | solution.py:154
  368.2 41.5 %all-to-all-start.1 = ((f32[32,3,32,128]{3,2,1,0:T(8,128)}), f32[32,3,32,128]{3,2,1,0:T(8,128)S(1)}, u32[]{:S(2)}, u32[]{:S(2)}) async-start(f32[32,3,32,128]{3,2,1,0:T(8,128)} %bitcast.16), calls=%async_computation.1 | async-start | bytes 3145728 | tf_op jit(solution)/shard_map/all_to_all | solution.py:154
  409.7 1.2 copy-start.1
